TPU v7x, 32 devices: a whole 2x2x4 slice. The times are simulated.
32 devices in a mesh: gz: 4 (over z), gy: 2 (over y), gx: 4 (over x, core).
Axes of the slice: x: 2, y: 2, z: 4, core: 2. Of those that a mesh axis runs over, the one named last changes fastest.
Arguments:
- velocity: float32 [3, 128, 32, 512], P(None, 'gx', 'gy', 'gz'), may hold values from -3.5 to 5.5
- pressure: float32 [128, 32, 512], P('gx', 'gy', 'gz'), may hold values from -6 to 6
- voidage: float32 [128, 32, 512], P('gx', 'gy', 'gz'), may hold values from 0.5 to 0.95
- particle_vel: float32 [3, 128, 32, 512], P(None, 'gx', 'gy', 'gz'), may hold values from -6 to 6
- forcing: float32 [1], replicated, may hold values from 0.5 to 2
- target_flux: float32 [1], replicated, may hold values from 0.5 to 1.5
Outputs:
- vel_new: float32 [3, 128, 32, 512], P(None, 'gx', 'gy', 'gz')
- source: float32 [128, 32, 512], P('gx', 'gy', 'gz')
- forcing_new: float32 [1], replicated
All inputs are finite; a program needn't handle non-finite values.
Results may differ from a plain program's by a relative error of at most 0.000079.
Values sent between devices are 32-bit elements; how exact they have to be, the bound alone decides.
A program may use at most 64 MiB of HBM per device.

v0:
```python
import jax
import jax.numpy as jnp
from jax import lax
from jax.sharding import PartitionSpec as P

time_step = 0.2
viscosity = 0.1
drag_scale = 1.0


def with_halo(block, sides, width):
    for axis, dim in sides:
        count = lax.axis_size(axis)
        forward = [(i, i + 1) for i in range(count - 1)]
        forward.append((count - 1, 0))
        backward = [(target, source) for source, target in forward]
        low = lax.ppermute(
            lax.slice_in_dim(block, block.shape[dim] - width, None, axis=dim), axis, forward
        )
        high = lax.ppermute(lax.slice_in_dim(block, 0, width, axis=dim), axis, backward)
        block = jnp.concatenate([low, block, high], axis=dim)
    return block


def shifted(field, axis_no, offset):
    slices = [slice(1, -1)] * 3
    length = field.shape[field.ndim - 3 + axis_no]
    slices[axis_no] = slice(1 + offset, length - 1 + offset)
    return field[tuple([slice(None)] * (field.ndim - 3) + slices)]


def upward():
    return (jnp.arange(3) == 2).astype(jnp.float32).reshape(3, 1, 1, 1)


def predict(vel_pad, pres_pad, voidage, particle_vel, forcing):
    centre = shifted(vel_pad, 0, 0)
    advection = jnp.zeros_like(centre)
    laplace = -6.0 * centre
    grads = []
    for axis_no in range(3):
        upper = shifted(vel_pad, axis_no, 1)
        lower = shifted(vel_pad, axis_no, -1)
        advection = advection + centre[axis_no] * (upper - lower) * 0.5
        laplace = laplace + upper + lower
        grads.append((shifted(pres_pad, axis_no, 1) - shifted(pres_pad, axis_no, -1)) * 0.5)
    forces = -advection + viscosity * laplace - jnp.stack(grads) + forcing * upward()
    slip_speed = jnp.sqrt(jnp.sum((centre - particle_vel) ** 2, axis=0))
    drag_rate = drag_scale * (1.0 - voidage) * voidage ** (-2.65) * (1.0 + slip_speed)
    return (centre + time_step * (forces + drag_rate * particle_vel)) / (
        1.0 + time_step * drag_rate
    )


def edge_fill(field, axis_no, depth, at_low, at_high):
    length = field.shape[axis_no]
    low_part = lax.slice_in_dim(field, 0, depth, axis=axis_no)
    inner = lax.slice_in_dim(field, depth, length - depth, axis=axis_no)
    high_part = lax.slice_in_dim(field, length - depth, length, axis=axis_no)
    first = lax.slice_in_dim(field, depth, depth + 1, axis=axis_no)
    last = lax.slice_in_dim(field, length - depth - 1, length - depth, axis=axis_no)
    low_part = jnp.where(at_low, first, low_part)
    high_part = jnp.where(at_high, last, high_part)
    return jnp.concatenate([low_part, inner, high_part], axis=axis_no)


def outside(length, depth, at_low, at_high):
    positions = jnp.arange(length)
    return at_low & (positions < depth) | at_high & (positions >= length - depth)


def wall_zero(field, depth, x_low, x_high, y_low, y_high):
    walls = (
        outside(field.shape[-3], depth, x_low, x_high)[:, None]
        | outside(field.shape[-2], depth, y_low, y_high)[None, :]
    )
    return jnp.where(walls[:, :, None], 0.0, field)


def local(velocity, pressure, voidage, particle_vel, forcing, target_flux):
    x_index = lax.axis_index("gx")
    x_low = x_index == 0
    x_high = x_index == lax.axis_size("gx") - 1
    y_index = lax.axis_index("gy")
    y_low = y_index == 0
    y_high = y_index == lax.axis_size("gy") - 1
    cells = voidage.size * lax.axis_size("gx") * lax.axis_size("gy") * lax.axis_size("gz")
    stacked = jnp.concatenate([velocity, pressure[None]], axis=0)
    padded = with_halo(stacked, (("gz", 3), ("gy", 2), ("gx", 1)), 1)
    vel_pad = wall_zero(padded[:3], 1, x_low, x_high, y_low, y_high)
    pres_pad = edge_fill(edge_fill(padded[3], 0, 1, x_low, x_high), 1, 1, y_low, y_high)
    ustar = predict(vel_pad, pres_pad, voidage, particle_vel, forcing[0])
    flux_stack = jnp.concatenate([voidage * ustar, voidage[None]], axis=0)
    flux_joined = with_halo(flux_stack, (("gz", 3), ("gy", 2), ("gx", 1)), 1)
    flux_pad = wall_zero(flux_joined, 1, x_low, x_high, y_low, y_high)
    divergence = jnp.zeros_like(voidage)
    for axis_no in range(3):
        divergence = (
            divergence
            + (shifted(flux_pad[axis_no], axis_no, 1) - shifted(flux_pad[axis_no], axis_no, -1))
            * 0.5
        )
    void_slope = (shifted(flux_pad[3], 2, 1) - shifted(flux_pad[3], 2, -1)) * 0.5
    flow_part = jnp.sum(voidage * ustar[2])
    flow_sum, void_sum = lax.psum((flow_part, jnp.sum(voidage)), ("gz", "gy", "gx"))
    force_step = (target_flux[0] * cells - flow_sum) / (time_step * void_sum)
    vel_new = ustar + time_step * force_step * upward()
    source = divergence + time_step * force_step * void_slope
    return (vel_new, source, forcing + force_step)


def solution(mesh):
    return jax.shard_map(
        local,
        mesh=mesh,
        in_specs=(
            P(None, "gx", "gy", "gz"),
            P("gx", "gy", "gz"),
            P("gx", "gy", "gz"),
            P(None, "gx", "gy", "gz"),
            P(),
            P(),
        ),
        out_specs=(P(None, "gx", "gy", "gz"), P("gx", "gy", "gz"), P()),
        check_vma=False,
    )
```

profile of v0, /device:TPU:0, one launch (start us, length us, event | category | flops | bytes accessed | tf_op | source)
XLA Modules:
  0.0 101.6 jit_solution(9995374795678290658)
XLA Ops:
  0.7 2.0 %fusion.1 = (f32[4,32,16,1]{3,2,1,0:T(8,128)S(1)}, f32[4,32,16,1]{3,2,1,0:T(8,128)S(1)}) fusion(f32[3,32,16,128]{3,2,1,0:T(8,128)} %param.6, f32[1,32,16,128]{3,2,1,0:T(8,128)} %bitcast.39), kind=kLoop, calls=%fused_computation.13 | loop fusion | flops 4096 | bytes 1064960 | tf_op jit(solution)/shard_map/concatenate | solution.py:88
  3.2 5.1 %collective-permute-start.1 = (f32[4,32,16,1]{1,2,3,0:T(8,128)S(1)}, f32[4,32,16,1]{1,2,3,0:T(8,128)S(1)}, u32[]{:S(2)}, u32[]{:S(2)}) collective-permute-start(f32[4,32,16,1]{1,2,3,0:T(8,128)S(1)} %copy.199), channel_id=1, source_target_pairs={{8,0},{16,8},{24,16},{0,24},{9,1},{17,9},{25,17},{1,25},{10,2},{18... | collective-permute-start | bytes 24584 | tf_op jit(solution)/shard_map/ppermute | solution.py:20
  9.7 0.8 copy.184
  10.8 3.7 %collective-permute-done = f32[4,32,16,1]{1,2,3,0:T(8,128)S(1)} collective-permute-done((f32[4,32,16,1]{1,2,3,0:T(8,128)S(1)}, f32[4,32,16,1]{1,2,3,0:T(8,128)S(1)}, u32[]{:S(2)}, u32[]{:S(2)}) %collective-permute-start) | collective-permute-done | bytes 8224 | tf_op jit(solution)/shard_map/ppermute | solution.py:17
  15.6 1.6 %collective-permute-start.2 = (f32[4,32,1,130]{3,1,2,0:T(8,128)S(1)}, f32[4,32,1,130]{3,1,2,0:T(8,128)S(1)}, u32[]{:S(2)}, u32[]{:S(2)}) collective-permute-start(f32[4,32,1,130]{3,1,2,0:T(8,128)S(1)} %get-tuple-element.35), channel_id=1, source_target_pairs={{0,4},{4,0},{1,5},{5,1},{2,6},{6,2},{3,7},{7,3},{8,12},{12,8},{9,1... | collective-permute-start | bytes 199688 | tf_op jit(solution)/shard_map/ppermute | solution.py:17
  17.7 3.2 %collective-permute-done.2 = f32[4,32,1,130]{3,1,2,0:T(8,128)S(1)} collective-permute-done((f32[4,32,1,130]{3,1,2,0:T(8,128)S(1)}, f32[4,32,1,130]{3,1,2,0:T(8,128)S(1)}, u32[]{:S(2)}, u32[]{:S(2)}) %collective-permute-start.2) | collective-permute-done | bytes 66592 | tf_op jit(solution)/shard_map/ppermute | solution.py:17
  20.9 1.4 %collective-permute-done.3 = f32[4,32,1,130]{3,1,2,0:T(8,128)S(1)} collective-permute-done((f32[4,32,1,130]{3,1,2,0:T(8,128)S(1)}, f32[4,32,1,130]{3,1,2,0:T(8,128)S(1)}, u32[]{:S(2)}, u32[]{:S(2)}) %collective-permute-start.3) | collective-permute-done | bytes 66592 | tf_op jit(solution)/shard_map/ppermute | solution.py:20
  23.7 1.2 %collective-permute-done.5 = f32[4,1,18,130]{3,0,2,1:T(4,128)S(1)} collective-permute-done((f32[4,1,18,130]{3,0,2,1:T(4,128)S(1)}, f32[4,1,18,130]{3,0,2,1:T(4,128)S(1)}, u32[]{:S(2)}, u32[]{:S(2)}) %collective-permute-start.5) | collective-permute-done | bytes 37472 | tf_op jit(solution)/shard_map/ppermute | solution.py:20
  24.9 2.5 %collective-permute-done.4 = f32[4,1,18,130]{3,0,2,1:T(4,128)S(1)} collective-permute-done((f32[4,1,18,130]{3,0,2,1:T(4,128)S(1)}, f32[4,1,18,130]{3,0,2,1:T(4,128)S(1)}, u32[]{:S(2)}, u32[]{:S(2)}) %collective-permute-start.4) | collective-permute-done | bytes 37472 | tf_op jit(solution)/shard_map/ppermute | solution.py:17
  27.9 1.0 fusion
  29.6 0.9 multiply_add_fusion
  31.2 1.6 %broadcast_multiply_fusion = (f32[3,32,16,128]{3,1,2,0:T(8,128)S(1)}, f32[3,32,16,128]{3,1,2,0:T(8,128)S(1)}) fusion(f32[32,16,128]{2,0,1:T(8,128)S(1)} %copy-done.5, f32[32,16,128]{2,0,1:T(8,128)S(1)} %copy.183, f32[3,32,16,128]{3,2,1,0:T(8,128)S(1)} %copy-done.2, f32[32,16,128]{2,0,1:T(8,128)S(1)} %copy.181, f32[3]{0:T(128)S(1)} %compare_select_fusion.1, ...), kind=kLoop, calls=%fused_computation.30 | loop fusion | flops 5701632 | bytes 10223628 | tf_op jit(solution)/shard_map/mul | solution.py:93
  33.6 1.4 %slice_maximum_fusion = (f32[4,32,16,1]{3,1,2,0:T(8,128)}, f32[4,32,16,1]{3,1,2,0:T(8,128)S(1)}) fusion(f32[1,32,16,128]{3,1,2,0:T(8,128)S(1)} %get-tuple-element.52, f32[3,32,16,128]{3,1,2,0:T(8,128)S(1)} %get-tuple-element.23), kind=kLoop, calls=%fused_computation.16 | loop fusion | flops 4096 | bytes 1064960 | tf_op jit(solution)/shard_map/concatenate | solution.py:93
  35.0 1.7 %copy.187 = f32[4,32,16,1]{1,2,3,0:T(8,128)S(1)} copy(f32[4,32,16,1]{3,1,2,0:T(8,128)} %get-tuple-element.44) | data formatting | bytes 16384 | tf_op jit(solution)/shard_map/slice | solution.py:18
  37.1 3.9 %collective-permute-start.7 = (f32[4,32,16,1]{1,2,3,0:T(8,128)S(1)}, f32[4,32,16,1]{1,2,3,0:T(8,128)S(1)}, u32[]{:S(2)}, u32[]{:S(2)}) collective-permute-start(f32[4,32,16,1]{1,2,3,0:T(8,128)S(1)} %copy.188), channel_id=1, source_target_pairs={{8,0},{16,8},{24,16},{0,24},{9,1},{17,9},{25,17},{1,25},{10,2},{18... | collective-permute-start | bytes 24584 | tf_op jit(solution)/shard_map/ppermute | solution.py:20
  41.6 37.3 %all-reduce = (f32[]{:T(128)}, f32[]{:T(128)}) all-reduce(f32[]{:T(128)} %get-tuple-element.53, f32[]{:T(128)} %get-tuple-element.54), channel_id=1, replica_groups=mesh['gz'=4,'gy'=2,'gx'=4] {'gz','gy','gx'}, use_global_device_ids=true, to_apply=%region_2.3 | all-reduce | flops 2 | bytes 16 | tf_op jit(solution)/shard_map/psum | solution.py:105
  81.4 2.6 %collective-permute-start.8 = (f32[4,32,1,130]{3,1,2,0:T(8,128)S(1)}, f32[4,32,1,130]{3,1,2,0:T(8,128)S(1)}, u32[]{:S(2)}, u32[]{:S(2)}) collective-permute-start(f32[4,32,1,130]{3,1,2,0:T(8,128)S(1)} %get-tuple-element.33), channel_id=1, source_target_pairs={{0,4},{4,0},{1,5},{5,1},{2,6},{6,2},{3,7},{7,3},{8,12},{12,8},{9,1... | collective-permute-start | bytes 199688 | tf_op jit(solution)/shard_map/ppermute | solution.py:17
  84.1 3.9 %collective-permute-done.8 = f32[4,32,1,130]{3,1,2,0:T(8,128)S(1)} collective-permute-done((f32[4,32,1,130]{3,1,2,0:T(8,128)S(1)}, f32[4,32,1,130]{3,1,2,0:T(8,128)S(1)}, u32[]{:S(2)}, u32[]{:S(2)}) %collective-permute-start.8) | collective-permute-done | bytes 66592 | tf_op jit(solution)/shard_map/ppermute | solution.py:17
  88.0 1.4 %collective-permute-done.9 = f32[4,32,1,130]{3,1,2,0:T(8,128)S(1)} collective-permute-done((f32[4,32,1,130]{3,1,2,0:T(8,128)S(1)}, f32[4,32,1,130]{3,1,2,0:T(8,128)S(1)}, u32[]{:S(2)}, u32[]{:S(2)}) %collective-permute-start.9) | collective-permute-done | bytes 66592 | tf_op jit(solution)/shard_map/ppermute | solution.py:20
  91.1 1.1 %broadcast_add_fusion = f32[3,32,16,128]{3,1,2,0:T(8,128)} fusion(f32[3,32,16,128]{3,1,2,0:T(8,128)S(1)} %copy-done.1, f32[3]{0:T(128)S(1)} %compare_select_fusion), kind=kLoop, calls=%fused_computation.31 | loop fusion | flops 196608 | bytes 1572876 | tf_op jit(solution)/shard_map/add | solution.py:107
  92.1 2.5 %copy.195 = f32[3,32,16,128]{3,2,1,0:T(8,128)} copy(f32[3,32,16,128]{3,1,2,0:T(8,128)} %broadcast_add_fusion) | data formatting | bytes 1572864
  94.6 1.0 copy.194
  95.7 3.2 %maximum_select_fusion = f32[4,34,18,130]{3,1,2,0:T(8,128)S(1)} fusion(f32[4,1,18,130]{3,1,2,0:T(1,128)S(1)} %copy.194, f32[4,32,1,130]{3,1,2,0:T(8,128)S(1)} %collective-permute-done.9, f32[4,32,16,1]{3,1,2,0:T(8,128)S(1)} %copy.190, f32[1,32,16,128]{3,1,2,0:T(8,128)S(1)} %get-tuple-element.52, f32[3,32,16,128]{3,1,2,0:T(8,128)S(1)} %get-tuple-element.23, ...), kind=kLoop, calls=%fused_computation | loop fusion | flops 2545920 | bytes 2546532 | tf_op jit(solution)/shard_map/jit(_where)/select_n | solution.py:77
  99.6 0.9 copy.196
  (67 shorter events, 11.2 us)
Async XLA Ops:
  0.6 8.3 %copy-start.3 = (f32[3,32,16,128]{3,2,1,0:T(8,128)S(1)}, f32[3,32,16,128]{3,2,1,0:T(8,128)}, u32[]{:S(2)}) copy-start(f32[3,32,16,128]{3,2,1,0:T(8,128)} %param.6) | copy-start | bytes 2359300
  0.6 8.3 %copy-start.6 = (f32[32,16,128]{2,1,0:T(8,128)S(1)}, f32[32,16,128]{2,1,0:T(8,128)}, u32[]{:S(2)}) copy-start(f32[32,16,128]{2,1,0:T(8,128)} %param.7) | copy-start | bytes 786436
  0.7 9.0 %copy-start.4 = (f32[32,16,128]{2,1,0:T(8,128)S(1)}, f32[32,16,128]{2,1,0:T(8,128)}, u32[]{:S(2)}) copy-start(f32[32,16,128]{2,1,0:T(8,128)} %param.8) | copy-start | bytes 786436
  3.2 11.8 %collective-permute-start.1 = (f32[4,32,16,1]{1,2,3,0:T(8,128)S(1)}, f32[4,32,16,1]{1,2,3,0:T(8,128)S(1)}, u32[]{:S(2)}, u32[]{:S(2)}) collective-permute-start(f32[4,32,16,1]{1,2,3,0:T(8,128)S(1)} %copy.199), channel_id=1, source_target_pairs={{8,0},{16,8},{24,16},{0,24},{9,1},{17,9},{25,17},{1,25},{10,2},{18... | collective-permute-start | bytes 24584 | tf_op jit(solution)/shard_map/ppermute | solution.py:20
  8.8 5.7 %collective-permute-start = (f32[4,32,16,1]{1,2,3,0:T(8,128)S(1)}, f32[4,32,16,1]{1,2,3,0:T(8,128)S(1)}, u32[]{:S(2)}, u32[]{:S(2)}) collective-permute-start(f32[4,32,16,1]{1,2,3,0:T(8,128)S(1)} %copy.198), channel_id=1, source_target_pairs={{0,8},{8,16},{16,24},{24,0},{1,9},{9,17},{17,25},{25,1},{2,10},{10... | collective-permute-start | bytes 24584 | tf_op jit(solution)/shard_map/ppermute | solution.py:17
  8.9 19.0 %copy-start.7 = (pred[34,18]{0,1:T(8,128)(4,1)}, pred[34,18]{0,1:T(8,128)(4,1)S(1)}, u32[]{:S(2)}) copy-start(pred[34,18]{0,1:T(8,128)(4,1)S(1)} %broadcast_or_fusion) | copy-start | bytes 1840
  15.6 5.3 %collective-permute-start.2 = (f32[4,32,1,130]{3,1,2,0:T(8,128)S(1)}, f32[4,32,1,130]{3,1,2,0:T(8,128)S(1)}, u32[]{:S(2)}, u32[]{:S(2)}) collective-permute-start(f32[4,32,1,130]{3,1,2,0:T(8,128)S(1)} %get-tuple-element.35), channel_id=1, source_target_pairs={{0,4},{4,0},{1,5},{5,1},{2,6},{6,2},{3,7},{7,3},{8,12},{12,8},{9,1... | collective-permute-start | bytes 199688 | tf_op jit(solution)/shard_map/ppermute | solution.py:17
  17.2 5.1 %collective-permute-start.3 = (f32[4,32,1,130]{3,1,2,0:T(8,128)S(1)}, f32[4,32,1,130]{3,1,2,0:T(8,128)S(1)}, u32[]{:S(2)}, u32[]{:S(2)}) collective-permute-start(f32[4,32,1,130]{3,1,2,0:T(8,128)S(1)} %get-tuple-element.36), channel_id=1, source_target_pairs={{4,0},{0,4},{5,1},{1,5},{6,2},{2,6},{7,3},{3,7},{12,8},{8,12},{13,... | collective-permute-start | bytes 199688 | tf_op jit(solution)/shard_map/ppermute | solution.py:20
  22.8 2.0 %collective-permute-start.5 = (f32[4,1,18,130]{3,0,2,1:T(4,128)S(1)}, f32[4,1,18,130]{3,0,2,1:T(4,128)S(1)}, u32[]{:S(2)}, u32[]{:S(2)}) collective-permute-start(f32[4,1,18,130]{3,0,2,1:T(4,128)S(1)} %copy.173), channel_id=1, source_target_pairs={{1,0},{2,1},{3,2},{0,3},{5,4},{6,5},{7,6},{4,7},{9,8},{10,9},{11,1... | collective-permute-start | bytes 112328 | tf_op jit(solution)/shard_map/ppermute | solution.py:20
  22.9 4.6 %collective-permute-start.4 = (f32[4,1,18,130]{3,0,2,1:T(4,128)S(1)}, f32[4,1,18,130]{3,0,2,1:T(4,128)S(1)}, u32[]{:S(2)}, u32[]{:S(2)}) collective-permute-start(f32[4,1,18,130]{3,0,2,1:T(4,128)S(1)} %copy.172), channel_id=1, source_target_pairs={{0,1},{1,2},{2,3},{3,0},{4,5},{5,6},{6,7},{7,4},{8,9},{9,10},{10,1... | collective-permute-start | bytes 112328 | tf_op jit(solution)/shard_map/ppermute | solution.py:17
  27.9 1.3 %copy-start.2 = (f32[3,32,16,128]{3,2,1,0:T(8,128)S(1)}, f32[3,32,16,128]{3,2,1,0:T(8,128)}, u32[]{:S(2)}) copy-start(f32[3,32,16,128]{3,2,1,0:T(8,128)} %param.9) | copy-start | bytes 2359300
  29.6 1.6 %copy-start.5 = (f32[32,16,128]{2,0,1:T(8,128)S(1)}, f32[32,16,128]{2,0,1:T(8,128)}, u32[]{:S(2)}) copy-start(f32[32,16,128]{2,0,1:T(8,128)} %copy.184) | copy-start | bytes 786436
  32.8 4.3 %copy-start = (f32[3,32,16,128]{3,1,2,0:T(8,128)}, f32[3,32,16,128]{3,1,2,0:T(8,128)S(1)}, u32[]{:S(2)}) copy-start(f32[3,32,16,128]{3,1,2,0:T(8,128)S(1)} %get-tuple-element.24) | copy-start | bytes 2359300
  36.6 43.7 %collective-permute-start.6 = (f32[4,32,16,1]{1,2,3,0:T(8,128)S(1)}, f32[4,32,16,1]{1,2,3,0:T(8,128)S(1)}, u32[]{:S(2)}, u32[]{:S(2)}) collective-permute-start(f32[4,32,16,1]{1,2,3,0:T(8,128)S(1)} %copy.187), channel_id=1, source_target_pairs={{0,8},{8,16},{16,24},{24,0},{1,9},{9,17},{17,25},{25,1},{2,10},{10... | collective-permute-start | bytes 24584 | tf_op jit(solution)/shard_map/ppermute | solution.py:17
  37.1 43.6 %collective-permute-start.7 = (f32[4,32,16,1]{1,2,3,0:T(8,128)S(1)}, f32[4,32,16,1]{1,2,3,0:T(8,128)S(1)}, u32[]{:S(2)}, u32[]{:S(2)}) collective-permute-start(f32[4,32,16,1]{1,2,3,0:T(8,128)S(1)} %copy.188), channel_id=1, source_target_pairs={{8,0},{16,8},{24,16},{0,24},{9,1},{17,9},{25,17},{1,25},{10,2},{18... | collective-permute-start | bytes 24584 | tf_op jit(solution)/shard_map/ppermute | solution.py:20
  81.2 9.8 %copy-start.1 = (f32[3,32,16,128]{3,1,2,0:T(8,128)S(1)}, f32[3,32,16,128]{3,1,2,0:T(8,128)}, u32[]{:S(2)}) copy-start(f32[3,32,16,128]{3,1,2,0:T(8,128)} %copy-done) | copy-start | bytes 2359300
  81.4 6.6 %collective-permute-start.8 = (f32[4,32,1,130]{3,1,2,0:T(8,128)S(1)}, f32[4,32,1,130]{3,1,2,0:T(8,128)S(1)}, u32[]{:S(2)}, u32[]{:S(2)}) collective-permute-start(f32[4,32,1,130]{3,1,2,0:T(8,128)S(1)} %get-tuple-element.33), channel_id=1, source_target_pairs={{0,4},{4,0},{1,5},{5,1},{2,6},{6,2},{3,7},{7,3},{8,12},{12,8},{9,1... | collective-permute-start | bytes 199688 | tf_op jit(solution)/shard_map/ppermute | solution.py:17
  84.0 5.4 %collective-permute-start.9 = (f32[4,32,1,130]{3,1,2,0:T(8,128)S(1)}, f32[4,32,1,130]{3,1,2,0:T(8,128)S(1)}, u32[]{:S(2)}, u32[]{:S(2)}) collective-permute-start(f32[4,32,1,130]{3,1,2,0:T(8,128)S(1)} %get-tuple-element.34), channel_id=1, source_target_pairs={{4,0},{0,4},{5,1},{1,5},{6,2},{2,6},{7,3},{3,7},{12,8},{8,12},{13,... | collective-permute-start | bytes 199688 | tf_op jit(solution)/shard_map/ppermute | solution.py:20
  90.5 4.0 %collective-permute-start.11 = (f32[4,1,18,130]{3,0,2,1:T(4,128)}, f32[4,1,18,130]{3,0,2,1:T(4,128)}, u32[]{:S(2)}, u32[]{:S(2)}) collective-permute-start(f32[4,1,18,130]{3,0,2,1:T(4,128)} %copy.192), channel_id=1, source_target_pairs={{1,0},{2,1},{3,2},{0,3},{5,4},{6,5},{7,6},{4,7},{9,8},{10,9},{11,1... | collective-permute-start | bytes 112328 | tf_op jit(solution)/shard_map/ppermute | solution.py:20
  90.6 5.0 %collective-permute-start.10 = (f32[4,1,18,130]{3,0,2,1:T(4,128)S(1)}, f32[4,1,18,130]{3,0,2,1:T(4,128)S(1)}, u32[]{:S(2)}, u32[]{:S(2)}) collective-permute-start(f32[4,1,18,130]{3,0,2,1:T(4,128)S(1)} %copy.191), channel_id=1, source_target_pairs={{0,1},{1,2},{2,3},{3,0},{4,5},{5,6},{6,7},{7,4},{8,9},{9,10},{10,1... | collective-permute-start | bytes 112328 | tf_op jit(solution)/shard_map/ppermute | solution.py:17
where the time goes:
time: 103 us; the launch traced here: 102 us
  blocking collectives  37.3 us (36%)
  waiting for transfers between devices  17.4 us (17%)
  other arithmetic  15.2 us (15%)
  starting transfers between devices  14.9 us (14%)
  local copies, waits for them, and re-layouts  12.1 us (12%)
  between operations  4.72 us (5%)
    psum x1, blocking collectives, local(): lax.psum((flow_part, jnp.sum(voidage)), ('gz', 'gy', 'gx'))  37.3 us
    ppermute x6, waiting for transfers between devices, with_halo(): lax.ppermute(lax.slice_in_dim(block, block.shape[dim] - width, None, axis...  13.4 us
    ppermute x6, starting transfers between devices, with_halo(): lax.ppermute(lax.slice_in_dim(block, 0, width, axis=dim), axis, backward)  9.61 us
    ppermute x6, starting transfers between devices, with_halo(): lax.ppermute(lax.slice_in_dim(block, block.shape[dim] - width, None, axis...  5.25 us
    unnamed x21, local copies, waits for them, and re-layouts  5.15 us
    select_n x2, other arithmetic, wall_zero(): return jnp.where(walls[:, :, None], 0.0, field)  4.19 us
    ppermute x6, waiting for transfers between devices, with_halo(): lax.ppermute(lax.slice_in_dim(block, 0, width, axis=dim), axis, backward)  4.02 us
    concatenate x2, other arithmetic, local(): stacked = jnp.concatenate([velocity, pressure[None]], axis=0)  2.08 us
  transfers between devices with their start and end apart: 12, of which 7 were waited for; matrix products, arithmetic and copies ran while one was open for 8% of the time, Pallas kernels for 0%

commit v1 on v0

v1 whole, which is shorter than its diff:
```python
import functools
import math

import jax
import jax.numpy as jnp
from jax import lax
from jax.experimental import pallas as pl
from jax.experimental.pallas import tpu as pltpu
from jax.sharding import PartitionSpec as P

time_step = 0.2
viscosity = 0.1
drag_scale = 1.0
MESH = pl.DeviceIdType.MESH
DIRECT_LIMIT = 0


def ring_index(axes):
    index = 0
    for axis in axes:
        index = index * lax.axis_size(axis) + lax.axis_index(axis)
    return index


def ring_device(axes, index):
    device = {}
    for axis in reversed(axes):
        size = lax.axis_size(axis)
        device[axis] = lax.rem(index, size)
        index = lax.div(index, size)
    return device


def kernel(
    sizes, phases,
    vel_hbm, pres_hbm, void_hbm, part_hbm, forcing, target,
    ustar, div, slope, step_out,
    blk, void, part, inv, flux, ypack, yhalo, zpack, zhalo,
    fypack, fyhalo, fxhalo, fzpack, fzhalo, slots,
    load_sem, send1, recv1, send2, recv2, sum_send, sum_recv,
):
    gx, gy, gz = sizes
    nx, ny, nz = div.shape
    x_at, y_at, z_at = (lax.axis_index(a) for a in ("gx", "gy", "gz"))
    not_low_x, not_high_x = x_at > 0, x_at < gx - 1
    not_low_y, not_high_y = y_at > 0, y_at < gy - 1
    z_up, z_down = lax.rem(z_at + 1, gz), lax.rem(z_at + gz - 1, gz)

    loads = [
        pltpu.make_async_copy(vel_hbm, blk.at[pl.ds(0, 3), pl.ds(1, nx)], load_sem.at[0]),
        pltpu.make_async_copy(pres_hbm, blk.at[3, pl.ds(1, nx)], load_sem.at[1]),
        pltpu.make_async_copy(void_hbm, void, load_sem.at[2]),
        pltpu.make_async_copy(part_hbm, part, load_sem.at[3]),
    ]
    for load in loads:
        load.start()

    barrier = pltpu.get_barrier_semaphore()
    peers = 0
    for axes in phases:
        count = math.prod(lax.axis_size(a) for a in axes)
        me = ring_index(axes)
        for k in range(1, count):
            pl.semaphore_signal(
                barrier, inc=1, device_id=ring_device(axes, lax.rem(me + k, count)),
                device_id_type=MESH,
            )
        peers += count - 1

    lane = lax.broadcasted_iota(jnp.int32, (ny, nz), 1)
    row = lax.broadcasted_iota(jnp.int32, (ny, nz), 0)

    def pack_z(fields, read, out):
        def body(x, carry):
            low, high = carry
            for f in range(fields):
                at = f * nx + x
                turned = pltpu.roll(read(f, x), at, 1)
                low = jnp.where(lane == at, turned, low)
                high = jnp.where(lane == lax.rem(at + nz - 1, nz), turned, high)
            return low, high

        zero = jnp.zeros((ny, nz), jnp.float32)
        low, high = lax.fori_loop(0, nx, body, (zero, zero), unroll=4)
        out[0] = low
        out[1] = high

    def copies(src_low, src_high, dst_low, dst_high, base, send, recv, axis, up, down):
        up_copy = pltpu.make_async_remote_copy(
            src_high, dst_low, send.at[base], recv.at[base],
            device_id={axis: up}, device_id_type=MESH)
        down_copy = pltpu.make_async_remote_copy(
            src_low, dst_high, send.at[base + 1], recv.at[base + 1],
            device_id={axis: down}, device_id_type=MESH)
        return up_copy, down_copy

    def start(pair, high, low):
        if high is None:
            pair[0].start()
            pair[1].start()
        else:
            pl.when(high)(pair[0].start)
            pl.when(low)(pair[1].start)

    def finish(pair, high, low):
        if high is None:
            pair[0].wait_recv()
            pair[1].wait_recv()
        else:
            pl.when(low)(pair[0].wait_recv)
            pl.when(high)(pair[1].wait_recv)

    def drain(pair, high, low):
        if high is None:
            pair[0].wait_send()
            pair[1].wait_send()
        else:
            pl.when(high)(pair[0].wait_send)
            pl.when(low)(pair[1].wait_send)

    up_x, down_x = jnp.minimum(x_at + 1, gx - 1), jnp.maximum(x_at - 1, 0)
    up_y, down_y = jnp.minimum(y_at + 1, gy - 1), jnp.maximum(y_at - 1, 0)

    loads[0].wait()
    loads[1].wait()
    for f in range(4):
        ypack[0, f] = blk[f, pl.ds(1, nx), 0, :]
        ypack[1, f] = blk[f, pl.ds(1, nx), ny - 1, :]
    pack_z(4, lambda f, x: blk[f, x + 1], zpack)
    pl.semaphore_wait(barrier, peers)

    y1 = copies(ypack.at[0], ypack.at[1], yhalo.at[0], yhalo.at[1], 0, send1, recv1, "gy", up_y, down_y)
    x1 = copies(blk.at[:, 1], blk.at[:, nx], blk.at[:, 0], blk.at[:, nx + 1], 2, send1, recv1, "gx", up_x, down_x)
    z1 = copies(zpack.at[0], zpack.at[1], zhalo.at[0], zhalo.at[1], 4, send1, recv1, "gz", z_up, z_down)
    start(z1, None, None)
    start(y1, not_high_y, not_low_y)
    start(x1, not_high_x, not_low_x)

    def wall_x(inside, halo_plane, edge_plane):
        @pl.when(jnp.logical_not(inside))
        def _():
            for f in range(3):
                blk[f, halo_plane] = jnp.zeros((ny, nz), jnp.float32)
            blk[3, halo_plane] = blk[3, edge_plane]

    wall_x(not_low_x, 0, 1)
    wall_x(not_high_x, nx + 1, nx)

    def wall_y(inside, side):
        @pl.when(jnp.logical_not(inside))
        def _():
            for f in range(3):
                yhalo[side, f] = jnp.zeros((nx, nz), jnp.float32)
            yhalo[side, 3] = ypack[side, 3]

    wall_y(not_low_y, 0)
    wall_y(not_high_y, 1)

    loads[2].wait()
    loads[3].wait()
    force = forcing[0]

    def plane(x):
        p = x + 1
        centre = [blk[f, p] for f in range(4)]
        v = void[x]
        q = [part[k, x] for k in range(3)]
        slip = jnp.sqrt(sum((centre[k] - q[k]) ** 2 for k in range(3)))
        drag = drag_scale * (1.0 - v) * jnp.exp(-2.65 * jnp.log(v)) * (1.0 + slip)
        inverse = 1.0 / (1.0 + time_step * drag)
        inv[x] = inverse

        def pair(f, axis_no):
            if axis_no == 0:
                return blk[f, p - 1], blk[f, p + 1]
            field = centre[f]
            if axis_no == 1:
                return (jnp.where(row == 0, 0.0, pltpu.roll(field, 1, 0)),
                        jnp.where(row == ny - 1, 0.0, pltpu.roll(field, ny - 1, 0)))
            return (jnp.where(lane == 0, 0.0, pltpu.roll(field, 1, 1)),
                    jnp.where(lane == nz - 1, 0.0, pltpu.roll(field, nz - 1, 1)))

        for k in range(3):
            advect = None
            total = None
            for axis_no in range(3):
                low, high = pair(k, axis_no)
                term = centre[axis_no] * (high - low)
                both = high + low
                advect = term if advect is None else advect + term
                total = both if total is None else total + both
            low, high = pair(3, k)
            forces = (viscosity * (total - 6.0 * centre[k])
                      - 0.5 * (advect + (high - low)))
            if k == 2:
                forces = forces + force
            ustar[k, x] = (centre[k] + time_step * (forces + drag * q[k])) * inverse

    def plane_body(i, carry):
        plane(1 + 2 * i)
        plane(2 + 2 * i)
        return carry

    lax.fori_loop(0, (nx - 2) // 2, plane_body, 0)

    finish(x1, not_high_x, not_low_x)
    plane(0)
    plane(nx - 1)

    finish(z1, None, None)
    finish(y1, not_high_y, not_low_y)

    first_row = row == 0
    last_row = row == ny - 1
    first_lane = lane == 0
    last_lane = lane == nz - 1
    row_sign = jnp.where(first_row, 1.0, jnp.where(last_row, -1.0, 0.0))
    lane_sign = jnp.where(first_lane, 1.0, jnp.where(last_lane, -1.0, 0.0))
    row_sign, lane_sign = (s * (0.5 * time_step) for s in (row_sign, lane_sign))
    row_visc, lane_visc = (jnp.abs(s) * (2.0 * viscosity) for s in (row_sign, lane_sign))

    def join_z(halo):
        low = pltpu.roll(halo[0], 1, 1)
        high = pltpu.roll(halo[1], nz - 1, 1)
        even = lax.rem(lane, 2) == 0
        return jnp.where(even, low, high), jnp.where(even, high, low)

    joined = join_z(zhalo)

    def unpack(which, at):
        return pltpu.roll(which, lax.rem(2 * nz - at, nz), 1)

    def correct(x, which, flow, void_total):
        inverse = inv[x]
        vy, vz = blk[1, x + 1], blk[2, x + 1]
        by_row = (row_visc + row_sign * vy) * inverse
        by_lane = (lane_visc + lane_sign * vz) * inverse

        def rows(f):
            return jnp.where(
                row < ny // 2,
                jnp.broadcast_to(yhalo[0, f, pl.ds(x, 1), :], (ny, nz)),
                jnp.broadcast_to(yhalo[1, f, pl.ds(x, 1), :], (ny, nz)))

        v = void[x]
        for k in range(3):
            value = ustar[k, x] + by_row * rows(k) + by_lane * unpack(which, k * nx + x)
            if k == 1:
                value = value + row_sign * inverse * rows(3)
            if k == 2:
                value = value + lane_sign * inverse * unpack(which, 3 * nx + x)
            ustar[k, x] = value
            moved = v * value
            flux[k, x] = moved
        return flow + moved, void_total + v

    def correct_body(i, carry):
        flow, void_total = carry
        flow, void_total = correct(2 * i, joined[0], flow, void_total)
        return correct(2 * i + 1, joined[1], flow, void_total)

    zero = jnp.zeros((ny, nz), jnp.float32)
    flow, void_total = lax.fori_loop(0, nx // 2, correct_body, (zero, zero))

    def fold(value):
        value = jnp.sum(value, axis=0, keepdims=True)
        return value + pltpu.roll(value, nz // 2, 1)

    line = lax.broadcasted_iota(jnp.int32, (1, nz), 1)
    partial = jnp.where(line < nz // 2, fold(flow), fold(void_total))

    def send_sum(which, value):
        axes = phases[which]
        count = math.prod(lax.axis_size(a) for a in axes)
        me = ring_index(axes)
        base = sum(math.prod(lax.axis_size(a) for a in phases[w]) for w in range(which))
        slots[base + me] = value
        out = []
        for k in range(1, count):
            out.append(pltpu.make_async_remote_copy(
                slots.at[base + me], slots.at[base + me],
                sum_send.at[base + k], sum_recv.at[base + me],
                device_id=ring_device(axes, lax.rem(me + k, count)), device_id_type=MESH))
            out[-1].start()
        return out

    def recv_sum(which):
        axes = phases[which]
        count = math.prod(lax.axis_size(a) for a in axes)
        me = ring_index(axes)
        base = sum(math.prod(lax.axis_size(a) for a in phases[w]) for w in range(which))
        for k in range(1, count):
            source = lax.rem(me + k, count)
            pltpu.make_async_remote_copy(
                slots.at[base + source], slots.at[base + source],
                sum_send.at[base + k], sum_recv.at[base + source],
                device_id=ring_device(axes, source), device_id_type=MESH).wait_recv()
        return jnp.sum(slots[pl.ds(base, count)], axis=0)

    sent = send_sum(0, partial)

    x2 = copies(flux.at[0, 0], flux.at[0, nx - 1], fxhalo.at[0], fxhalo.at[1], 0, send2, recv2, "gx", up_x, down_x)
    y2 = copies(fypack.at[0], fypack.at[1], fyhalo.at[0], fyhalo.at[1], 2, send2, recv2, "gy", up_y, down_y)
    z2 = copies(fzpack.at[0], fzpack.at[1], fzhalo.at[0], fzhalo.at[1], 4, send2, recv2, "gz", z_up, z_down)
    start(x2, not_high_x, not_low_x)
    fypack[0] = flux[1, :, 0, :]
    fypack[1] = flux[1, :, ny - 1, :]
    start(y2, not_high_y, not_low_y)
    pack_z(2, lambda f, x: flux[2, x] if f == 0 else void[x], fzpack)
    start(z2, None, None)

    for inside, side in ((not_low_x, 0), (not_high_x, 1)):
        @pl.when(jnp.logical_not(inside))
        def _():
            fxhalo[side] = jnp.zeros((ny, nz), jnp.float32)
    for inside, side in ((not_low_y, 0), (not_high_y, 1)):
        @pl.when(jnp.logical_not(inside))
        def _():
            fyhalo[side] = jnp.zeros((nx, nz), jnp.float32)

    phase = 0
    while phase < len(phases) - 1:
        total = recv_sum(phase)
        phase += 1
        sent += send_sum(phase, total)

    finish(x2, not_high_x, not_low_x)
    finish(y2, not_high_y, not_low_y)
    finish(z2, None, None)
    fz_joined = join_z(fzhalo)

    def source_plane(x, which, x_low, x_high):
        fy, fz, v = flux[1, x], flux[2, x], void[x]
        y_low = jnp.where(first_row, jnp.broadcast_to(fyhalo[0, pl.ds(x, 1), :], (ny, nz)), pltpu.roll(fy, 1, 0))
        y_high = jnp.where(last_row, jnp.broadcast_to(fyhalo[1, pl.ds(x, 1), :], (ny, nz)), pltpu.roll(fy, ny - 1, 0))
        z_halo, v_halo = unpack(which, x), unpack(which, nx + x)
        z_low = jnp.where(first_lane, z_halo, pltpu.roll(fz, 1, 1))
        z_high = jnp.where(last_lane, z_halo, pltpu.roll(fz, nz - 1, 1))
        v_low = jnp.where(first_lane, v_halo, pltpu.roll(v, 1, 1))
        v_high = jnp.where(last_lane, v_halo, pltpu.roll(v, nz - 1, 1))
        div[x] = 0.5 * ((x_high - x_low) + (y_high - y_low) + (z_high - z_low))
        slope[x] = (0.5 * time_step) * (v_high - v_low)

    source_plane(0, fz_joined[0], fxhalo[0], flux[0, 1])

    def source_body(i, carry):
        x = 2 * i + 1
        source_plane(x, fz_joined[1], flux[0, x - 1], flux[0, x + 1])
        source_plane(x + 1, fz_joined[0], flux[0, x], flux[0, x + 2])
        return carry

    lax.fori_loop(0, nx // 2 - 1, source_body, 0)
    source_plane(nx - 1, fz_joined[1], flux[0, nx - 2], fxhalo[1])

    total = recv_sum(phase)
    half = line < nz // 2
    flow_sum = jnp.sum(jnp.where(half, total, 0.0), axis=1, keepdims=True)
    void_sum = jnp.sum(jnp.where(half, 0.0, total), axis=1, keepdims=True)
    cells = float(nx * ny * nz * gx * gy * gz)
    step_out[...] = jnp.broadcast_to(
        (target[0] * cells - flow_sum) / (time_step * void_sum), (1, nz))

    for copy in sent:
        copy.wait_send()
    for pair, high, low in ((x1, not_high_x, not_low_x), (y1, not_high_y, not_low_y), (z1, None, None),
                            (x2, not_high_x, not_low_x), (y2, not_high_y, not_low_y), (z2, None, None)):
        drain(pair, high, low)


def local(velocity, pressure, voidage, particle_vel, forcing, target_flux):
    nx, ny, nz = voidage.shape
    sizes = tuple(lax.axis_size(a) for a in ("gx", "gy", "gz"))
    if math.prod(sizes) <= DIRECT_LIMIT:
        phases = (("gz", "gy", "gx"),)
    else:
        phases = (("gy", "gx"), ("gz",))
    slot_count = sum(math.prod(lax.axis_size(a) for a in axes) for axes in phases)
    f32 = jnp.float32
    vmem = pl.BlockSpec(memory_space=pltpu.VMEM)
    smem = pl.BlockSpec(memory_space=pltpu.SMEM)
    hbm = pl.BlockSpec(memory_space=pl.ANY)
    dma = pltpu.SemaphoreType.DMA
    ustar, div, slope, step = pl.pallas_call(
        functools.partial(kernel, sizes, phases),
        out_shape=(
            jax.ShapeDtypeStruct((3, nx, ny, nz), f32),
            jax.ShapeDtypeStruct((nx, ny, nz), f32),
            jax.ShapeDtypeStruct((nx, ny, nz), f32),
            jax.ShapeDtypeStruct((1, nz), f32),
        ),
        in_specs=[hbm, hbm, hbm, hbm, smem, smem],
        out_specs=(vmem, vmem, vmem, vmem),
        scratch_shapes=[
            pltpu.VMEM((4, nx + 2, ny, nz), f32),
            pltpu.VMEM((nx, ny, nz), f32),
            pltpu.VMEM((3, nx, ny, nz), f32),
            pltpu.VMEM((nx, ny, nz), f32),
            pltpu.VMEM((3, nx, ny, nz), f32),
            pltpu.VMEM((2, 4, nx, nz), f32),
            pltpu.VMEM((2, 4, nx, nz), f32),
            pltpu.VMEM((2, ny, nz), f32),
            pltpu.VMEM((2, ny, nz), f32),
            pltpu.VMEM((2, nx, nz), f32),
            pltpu.VMEM((2, nx, nz), f32),
            pltpu.VMEM((2, ny, nz), f32),
            pltpu.VMEM((2, ny, nz), f32),
            pltpu.VMEM((2, ny, nz), f32),
            pltpu.VMEM((slot_count, 1, nz), f32),
            dma((4,)), dma((6,)), dma((6,)), dma((6,)), dma((6,)),
            dma((slot_count,)), dma((slot_count,)),
        ],
        compiler_params=pltpu.CompilerParams(collective_id=0, has_side_effects=True),
    )(velocity, pressure, voidage, particle_vel, forcing, target_flux)
    force_step = step[0, :1]
    upward = (jnp.arange(3) == 2).astype(f32).reshape(3, 1, 1, 1)
    return (ustar + time_step * force_step[0] * upward, div + force_step[0] * slope, forcing + force_step)


def solution(mesh):
    return jax.shard_map(
        local,
        mesh=mesh,
        in_specs=(
            P(None, "gx", "gy", "gz"),
            P("gx", "gy", "gz"),
            P("gx", "gy", "gz"),
            P(None, "gx", "gy", "gz"),
            P(),
            P(),
        ),
        out_specs=(P(None, "gx", "gy", "gz"), P("gx", "gy", "gz"), P()),
        check_vma=False,
    )
```

time: 103 us -> 26.4 us (0.26); the launches traced: 102 us -> 26.2 us
  blocking collectives: 37.3 us -> 0 us
  Pallas kernels: 0 us -> 19.6 us
  waiting for transfers between devices: 17.4 us -> 0 us
  starting transfers between devices: 14.9 us -> 0 us
  local copies, waits for them, and re-layouts: 12.1 us -> 0.01 us
  other arithmetic: 15.2 us -> 3.43 us
  between operations: 4.72 us -> 3.17 us
    psum x1 -> x0, blocking collectives: 37.3 us -> none  [local(): lax.psum((flow_part, jnp.sum(voidage)), ('gz', 'gy', 'gx'))]
    pallas_call x0 -> x1, Pallas kernels: none -> 19.6 us  [local(): pl.pallas_call(functools.partial(kernel, sizes, phases), out_shape=(jax.S...]
    ppermute x12 -> x0, waiting for transfers between devices: 17.4 us -> none  [the longest x6 13.4 us: with_halo(): lax.ppermute(lax.slice_in_dim(block, block.shape[dim] - width, None, axis...]
    ppermute x12 -> x0, starting transfers between devices: 14.9 us -> none  [the longest x6 9.61 us: with_halo(): lax.ppermute(lax.slice_in_dim(block, 0, width, axis=dim), axis, backward)]
    unnamed x21 -> x4, local copies, waits for them, and re-layouts: 5.15 us -> 0.01 us
    select_n x4 -> x0, other arithmetic: 4.39 us -> none  [the longest x2 4.19 us: wall_zero(): return jnp.where(walls[:, :, None], 0.0, field)]
    concatenate x4 -> x0, other arithmetic: 3.57 us -> none  [the longest x2 2.08 us: local(): stacked = jnp.concatenate([velocity, pressure[None]], axis=0)]
    ppermute x8 -> x0, local copies, waits for them, and re-layouts: 3.02 us -> none  [the longest x4 1.95 us: with_halo(): lax.ppermute(lax.slice_in_dim(block, 0, width, axis=dim), axis, backward)]
  transfers between devices with their start and end apart: 12 -> 0, of which waited for: 7 -> 0; matrix products, arithmetic and copies ran while one was open for 8% -> 0% of each run, Pallas kernels for 0% -> 0%
where the time goes in v1:
time: 26.4 us; the launch traced here: 26.2 us
  Pallas kernels  19.6 us (74%)
  other arithmetic  3.43 us (13%)
  between operations  3.17 us (12%)
    pallas_call x1, Pallas kernels, local(): pl.pallas_call(functools.partial(kernel, sizes, phases), out_shape=(jax.S...  19.6 us
    add x1, other arithmetic, local(): div + force_step[0] * slope  2.41 us
    add x1, other arithmetic, local(): ustar + time_step * force_step[0] * upward  1.02 us

profile of v1, /device:TPU:0, one launch (start us, length us, event | category | flops | bytes accessed | tf_op | source)
XLA Modules:
  0.0 26.2 jit_solution(18339947025621846303)
XLA Ops:
  1.9 19.6 %shard_map.85 = (f32[3,32,16,128]{3,2,1,0:T(8,128)}, f32[32,16,128]{2,1,0:T(8,128)}, f32[32,16,128]{2,1,0:T(8,128)}, f32[1,128]{1,0:T(1,128)}) custom-call(f32[3,32,16,128]{3,2,1,0:T(8,128)} %vel_hbm.1, f32[32,16,128]{2,1,0:T(8,128)} %pres_hbm.1, f32[32,16,128]{2,1,0:T(8,128)} %void_hbm.1, f32[3,32,16,128]{3,2,1,0:T(8,128)} %part_hbm.1, f32[1]{0:T(128)S(6)} %copy.9.forcing, ...), custom_call_target="tpu_custom_call" | custom-call | tf_op jit(solution)/shard_map/pallas_call | solution.py:383
  21.5 0.0 copy-start
  21.5 0.0 copy-start.1
  21.5 2.4 %multiply_add_fusion = f32[32,16,128]{2,1,0:T(8,128)} fusion(f32[32,16,128]{2,1,0:T(8,128)} %get-tuple-element.9, f32[32,16,128]{2,1,0:T(8,128)} %get-tuple-element.10, f32[]{:T(128)} %bitcast.3), kind=kLoop, calls=%fused_computation.1 | loop fusion | flops 131072 | bytes 786436 | tf_op jit(solution)/shard_map/add | solution.py:416
  23.9 0.0 copy-done.1
  24.0 0.0 copy-done
  24.0 1.0 %broadcast_add_fusion = f32[3,32,16,128]{3,2,1,0:T(8,128)} fusion(f32[3,32,16,128]{3,2,1,0:T(8,128)S(1)} %copy-done, f32[3]{0:T(128)S(1)} %compare_select_fusion), kind=kLoop, calls=%fused_computation | loop fusion | flops 196608 | bytes 1572876 | tf_op jit(solution)/shard_map/add | solution.py:416
  (1 shorter events, 0.0 us)
Async XLA Ops:
  21.5 2.5 %copy-start = (f32[3,32,16,128]{3,2,1,0:T(8,128)S(1)}, f32[3,32,16,128]{3,2,1,0:T(8,128)}, u32[]{:S(2)}) copy-start(f32[3,32,16,128]{3,2,1,0:T(8,128)} %get-tuple-element.7) | copy-start | bytes 2359300
  21.5 2.4 %copy-start.1 = (f32[1,128]{1,0:T(1,128)S(1)}, f32[1,128]{1,0:T(1,128)}, u32[]{:S(2)}) copy-start(f32[1,128]{1,0:T(1,128)} %get-tuple-element.8) | copy-start | bytes 1540

commit v2 on v1

--- a/solution.py
+++ b/solution.py
@@ -12,7 +12,7 @@
 viscosity = 0.1
 drag_scale = 1.0
 MESH = pl.DeviceIdType.MESH
-DIRECT_LIMIT = 0
+DIRECT_LIMIT = 64
 
 
 def ring_index(axes):
@@ -33,10 +33,11 @@
 
 def kernel(
     sizes, phases,
-    vel_hbm, pres_hbm, void_hbm, part_hbm, forcing, target,
-    ustar, div, slope, step_out,
+    vel_hbm, pres_hbm, void_hbm, part_hbm, forcing_hbm, target_hbm,
+    ustar, div, step_out,
+    forcing, target, slope,
     blk, void, part, inv, flux, ypack, yhalo, zpack, zhalo,
-    fypack, fyhalo, fxhalo, fzpack, fzhalo, slots,
+    fypack, fyhalo, fxhalo, fzpack, fzhalo, vzpack, vzhalo, slots,
     load_sem, send1, recv1, send2, recv2, sum_send, sum_recv,
 ):
     gx, gy, gz = sizes
@@ -51,6 +52,8 @@
         pltpu.make_async_copy(pres_hbm, blk.at[3, pl.ds(1, nx)], load_sem.at[1]),
         pltpu.make_async_copy(void_hbm, void, load_sem.at[2]),
         pltpu.make_async_copy(part_hbm, part, load_sem.at[3]),
+        pltpu.make_async_copy(forcing_hbm, forcing, load_sem.at[4]),
+        pltpu.make_async_copy(target_hbm, target, load_sem.at[5]),
     ]
     for load in loads:
         load.start()
@@ -158,6 +161,8 @@
 
     loads[2].wait()
     loads[3].wait()
+    loads[4].wait()
+    loads[5].wait()
     force = forcing[0]
 
     def plane(x):
@@ -203,6 +208,10 @@
 
     lax.fori_loop(0, (nx - 2) // 2, plane_body, 0)
 
+    pack_z(1, lambda f, x: void[x], vzpack)
+    zv = copies(vzpack.at[0], vzpack.at[1], vzhalo.at[0], vzhalo.at[1], 6, send1, recv1, "gz", z_up, z_down)
+    start(zv, None, None)
+
     finish(x1, not_high_x, not_low_x)
     plane(0)
     plane(nx - 1)
@@ -230,37 +239,42 @@
     def unpack(which, at):
         return pltpu.roll(which, lax.rem(2 * nz - at, nz), 1)
 
-    def correct(x, which, flow, void_total):
-        inverse = inv[x]
-        vy, vz = blk[1, x + 1], blk[2, x + 1]
-        by_row = (row_visc + row_sign * vy) * inverse
-        by_lane = (lane_visc + lane_sign * vz) * inverse
-
-        def rows(f):
-            return jnp.where(
-                row < ny // 2,
-                jnp.broadcast_to(yhalo[0, f, pl.ds(x, 1), :], (ny, nz)),
-                jnp.broadcast_to(yhalo[1, f, pl.ds(x, 1), :], (ny, nz)))
-
-        v = void[x]
-        for k in range(3):
-            value = ustar[k, x] + by_row * rows(k) + by_lane * unpack(which, k * nx + x)
+    def rows(f, x):
+        return jnp.where(
+            row < ny // 2,
+            jnp.broadcast_to(yhalo[0, f, pl.ds(x, 1), :], (ny, nz)),
+            jnp.broadcast_to(yhalo[1, f, pl.ds(x, 1), :], (ny, nz)))
+
+    def correct(x, which, fields):
+        by_row = row_visc + row_sign * blk[1, x + 1]
+        by_lane = lane_visc + lane_sign * blk[2, x + 1]
+        inverse, v = inv[x], void[x]
+        for k in fields:
+            value = by_row * rows(k, x) + by_lane * unpack(which, k * nx + x)
             if k == 1:
-                value = value + row_sign * inverse * rows(3)
+                value = value + row_sign * rows(3, x)
             if k == 2:
-                value = value + lane_sign * inverse * unpack(which, 3 * nx + x)
+                value = value + lane_sign * unpack(which, 3 * nx + x)
+            value = ustar[k, x] + value * inverse
             ustar[k, x] = value
             moved = v * value
             flux[k, x] = moved
-        return flow + moved, void_total + v
-
-    def correct_body(i, carry):
+        return moved, v
+
+    def flow_body(i, carry):
         flow, void_total = carry
-        flow, void_total = correct(2 * i, joined[0], flow, void_total)
-        return correct(2 * i + 1, joined[1], flow, void_total)
+        for x, which in ((2 * i, joined[0]), (2 * i + 1, joined[1])):
+            moved, v = correct(x, which, (2,))
+            flow, void_total = flow + moved, void_total + v
+        return flow, void_total
+
+    def across_body(i, carry):
+        correct(2 * i, joined[0], (0, 1))
+        correct(2 * i + 1, joined[1], (0, 1))
+        return carry
 
     zero = jnp.zeros((ny, nz), jnp.float32)
-    flow, void_total = lax.fori_loop(0, nx // 2, correct_body, (zero, zero))
+    flow, void_total = lax.fori_loop(0, nx // 2, flow_body, (zero, zero))
 
     def fold(value):
         value = jnp.sum(value, axis=0, keepdims=True)
@@ -302,12 +316,13 @@
     x2 = copies(flux.at[0, 0], flux.at[0, nx - 1], fxhalo.at[0], fxhalo.at[1], 0, send2, recv2, "gx", up_x, down_x)
     y2 = copies(fypack.at[0], fypack.at[1], fyhalo.at[0], fyhalo.at[1], 2, send2, recv2, "gy", up_y, down_y)
     z2 = copies(fzpack.at[0], fzpack.at[1], fzhalo.at[0], fzhalo.at[1], 4, send2, recv2, "gz", z_up, z_down)
+    pack_z(1, lambda f, x: flux[2, x], fzpack)
+    start(z2, None, None)
+    lax.fori_loop(0, nx // 2, across_body, 0)
     start(x2, not_high_x, not_low_x)
     fypack[0] = flux[1, :, 0, :]
     fypack[1] = flux[1, :, ny - 1, :]
     start(y2, not_high_y, not_low_y)
-    pack_z(2, lambda f, x: flux[2, x] if f == 0 else void[x], fzpack)
-    start(z2, None, None)
 
     for inside, side in ((not_low_x, 0), (not_high_x, 1)):
         @pl.when(jnp.logical_not(inside))
@@ -327,13 +342,15 @@
     finish(x2, not_high_x, not_low_x)
     finish(y2, not_high_y, not_low_y)
     finish(z2, None, None)
+    finish(zv, None, None)
     fz_joined = join_z(fzhalo)
-
-    def source_plane(x, which, x_low, x_high):
+    vz_joined = join_z(vzhalo)
+
+    def source_plane(x, odd, x_low, x_high):
         fy, fz, v = flux[1, x], flux[2, x], void[x]
         y_low = jnp.where(first_row, jnp.broadcast_to(fyhalo[0, pl.ds(x, 1), :], (ny, nz)), pltpu.roll(fy, 1, 0))
         y_high = jnp.where(last_row, jnp.broadcast_to(fyhalo[1, pl.ds(x, 1), :], (ny, nz)), pltpu.roll(fy, ny - 1, 0))
-        z_halo, v_halo = unpack(which, x), unpack(which, nx + x)
+        z_halo, v_halo = unpack(fz_joined[odd], x), unpack(vz_joined[odd], x)
         z_low = jnp.where(first_lane, z_halo, pltpu.roll(fz, 1, 1))
         z_high = jnp.where(last_lane, z_halo, pltpu.roll(fz, nz - 1, 1))
         v_low = jnp.where(first_lane, v_halo, pltpu.roll(v, 1, 1))
@@ -341,28 +358,36 @@
         div[x] = 0.5 * ((x_high - x_low) + (y_high - y_low) + (z_high - z_low))
         slope[x] = (0.5 * time_step) * (v_high - v_low)
 
-    source_plane(0, fz_joined[0], fxhalo[0], flux[0, 1])
+    source_plane(0, 0, fxhalo[0], flux[0, 1])
 
     def source_body(i, carry):
         x = 2 * i + 1
-        source_plane(x, fz_joined[1], flux[0, x - 1], flux[0, x + 1])
-        source_plane(x + 1, fz_joined[0], flux[0, x], flux[0, x + 2])
+        source_plane(x, 1, flux[0, x - 1], flux[0, x + 1])
+        source_plane(x + 1, 0, flux[0, x], flux[0, x + 2])
         return carry
 
     lax.fori_loop(0, nx // 2 - 1, source_body, 0)
-    source_plane(nx - 1, fz_joined[1], flux[0, nx - 2], fxhalo[1])
+    source_plane(nx - 1, 1, flux[0, nx - 2], fxhalo[1])
 
     total = recv_sum(phase)
     half = line < nz // 2
     flow_sum = jnp.sum(jnp.where(half, total, 0.0), axis=1, keepdims=True)
     void_sum = jnp.sum(jnp.where(half, 0.0, total), axis=1, keepdims=True)
     cells = float(nx * ny * nz * gx * gy * gz)
-    step_out[...] = jnp.broadcast_to(
-        (target[0] * cells - flow_sum) / (time_step * void_sum), (1, nz))
+    step = (target[0] * cells - flow_sum) / (time_step * void_sum)
+    step_out[...] = jnp.broadcast_to(step, (1, nz)) + forcing[0]
+    step = jnp.broadcast_to(step, (ny, nz))
+
+    def final_body(x, carry):
+        ustar[2, x] = ustar[2, x] + time_step * step
+        div[x] = div[x] + step * slope[x]
+        return carry
+
+    lax.fori_loop(0, nx, final_body, 0, unroll=4)
 
     for copy in sent:
         copy.wait_send()
-    for pair, high, low in ((x1, not_high_x, not_low_x), (y1, not_high_y, not_low_y), (z1, None, None),
+    for pair, high, low in ((x1, not_high_x, not_low_x), (y1, not_high_y, not_low_y), (z1, None, None), (zv, None, None),
                             (x2, not_high_x, not_low_x), (y2, not_high_y, not_low_y), (z2, None, None)):
         drain(pair, high, low)
 
@@ -377,20 +402,21 @@
     slot_count = sum(math.prod(lax.axis_size(a) for a in axes) for axes in phases)
     f32 = jnp.float32
     vmem = pl.BlockSpec(memory_space=pltpu.VMEM)
-    smem = pl.BlockSpec(memory_space=pltpu.SMEM)
-    hbm = pl.BlockSpec(memory_space=pl.ANY)
+    hbm = pl.BlockSpec(memory_space=pltpu.HBM)
     dma = pltpu.SemaphoreType.DMA
-    ustar, div, slope, step = pl.pallas_call(
+    vel_new, source, forcing_new = pl.pallas_call(
         functools.partial(kernel, sizes, phases),
         out_shape=(
-            jax.ShapeDtypeStruct((3, nx, ny, nz), f32),
-            jax.ShapeDtypeStruct((nx, ny, nz), f32),
-            jax.ShapeDtypeStruct((nx, ny, nz), f32),
-            jax.ShapeDtypeStruct((1, nz), f32),
+            pltpu.VMEM((3, nx, ny, nz), f32),
+            pltpu.VMEM((nx, ny, nz), f32),
+            pltpu.VMEM((1, nz), f32),
         ),
-        in_specs=[hbm, hbm, hbm, hbm, smem, smem],
-        out_specs=(vmem, vmem, vmem, vmem),
+        in_specs=[hbm] * 6,
+        out_specs=(vmem,) * 3,
         scratch_shapes=[
+            pltpu.SMEM((1,), f32),
+            pltpu.SMEM((1,), f32),
+            pltpu.VMEM((nx, ny, nz), f32),
             pltpu.VMEM((4, nx + 2, ny, nz), f32),
             pltpu.VMEM((nx, ny, nz), f32),
             pltpu.VMEM((3, nx, ny, nz), f32),
@@ -405,15 +431,15 @@
             pltpu.VMEM((2, ny, nz), f32),
             pltpu.VMEM((2, ny, nz), f32),
             pltpu.VMEM((2, ny, nz), f32),
+            pltpu.VMEM((2, ny, nz), f32),
+            pltpu.VMEM((2, ny, nz), f32),
             pltpu.VMEM((slot_count, 1, nz), f32),
-            dma((4,)), dma((6,)), dma((6,)), dma((6,)), dma((6,)),
+            dma((6,)), dma((8,)), dma((8,)), dma((6,)), dma((6,)),
             dma((slot_count,)), dma((slot_count,)),
         ],
         compiler_params=pltpu.CompilerParams(collective_id=0, has_side_effects=True),
     )(velocity, pressure, voidage, particle_vel, forcing, target_flux)
-    force_step = step[0, :1]
-    upward = (jnp.arange(3) == 2).astype(f32).reshape(3, 1, 1, 1)
-    return (ustar + time_step * force_step[0] * upward, div + force_step[0] * slope, forcing + force_step)
+    return vel_new, source, forcing_new[0, :1]
 
 
 def solution(mesh):

time: 26.4 us -> 24.4 us (0.924)
  other arithmetic: 3.43 us -> 0 us
  local copies, waits for them, and re-layouts: 0.01 us -> 1.58 us
    add x2 -> x0, other arithmetic: 3.43 us -> none  [the longest x1 2.41 us: local(): div + force_step[0] * slope]
    unnamed x4 -> x2, local copies, waits for them, and re-layouts: 0.01 us -> 1.58 us
where the time goes in v2:
time: 24.4 us; the launch traced here: 24.2 us
  Pallas kernels  19.5 us (80%)
  between operations  3.1 us (13%)
  local copies, waits for them, and re-layouts  1.58 us (6%)
    pallas_call x1, Pallas kernels, local(): pl.pallas_call(functools.partial(kernel, sizes, phases), out_shape=(pltpu...  19.5 us
    unnamed x2, local copies, waits for them, and re-layouts  1.58 us

profile of v2, /device:TPU:0, one launch (start us, length us, event | category | flops | bytes accessed | tf_op | source)
XLA Modules:
  0.0 24.2 jit_solution(4525620373256023098)
XLA Ops:
  1.9 19.5 %shard_map.85 = (f32[3,32,16,128]{3,2,1,0:T(8,128)S(1)}, f32[32,16,128]{2,1,0:T(8,128)S(1)}, f32[1,128]{1,0:T(1,128)S(1)}) custom-call(f32[3,32,16,128]{3,2,1,0:T(8,128)} %vel_hbm.1, f32[32,16,128]{2,1,0:T(8,128)} %pres_hbm.1, f32[32,16,128]{2,1,0:T(8,128)} %void_hbm.1, f32[3,32,16,128]{3,2,1,0:T(8,128)} %part_hbm.1, f32[1]{0:T(128)S(6)} %copy.14.forcing_hbm, ...), custom_call_target="tpu_custom_call" | custom-call | tf_op jit(solution)/shard_map/pallas_call | solution.py:407
  21.4 0.9 %copy.12 = f32[3,32,16,128]{3,2,1,0:T(8,128)} copy(f32[3,32,16,128]{3,2,1,0:T(8,128)S(1)} %get-tuple-element.9) | data formatting | bytes 1572864
  22.3 0.7 %copy.13 = f32[32,16,128]{2,1,0:T(8,128)} copy(f32[32,16,128]{2,1,0:T(8,128)S(1)} %get-tuple-element.10) | data formatting | bytes 524288

commit v3 on v2

--- a/solution.py
+++ b/solution.py
@@ -32,13 +32,13 @@
 
 
 def kernel(
-    sizes, phases,
+    sizes, greet, phases,
     vel_hbm, pres_hbm, void_hbm, part_hbm, forcing_hbm, target_hbm,
     ustar, div, step_out,
     forcing, target, slope,
     blk, void, part, inv, flux, ypack, yhalo, zpack, zhalo,
     fypack, fyhalo, fxhalo, fzpack, fzhalo, vzpack, vzhalo, slots,
-    load_sem, send1, recv1, send2, recv2, sum_send, sum_recv,
+    load_sem, send1, recv1, send2, recv2, sum_send, sum_recv, entered,
 ):
     gx, gy, gz = sizes
     nx, ny, nz = div.shape
@@ -60,7 +60,7 @@
 
     barrier = pltpu.get_barrier_semaphore()
     peers = 0
-    for axes in phases:
+    for axes in greet:
         count = math.prod(lax.axis_size(a) for a in axes)
         me = ring_index(axes)
         for k in range(1, count):
@@ -130,35 +130,6 @@
         ypack[0, f] = blk[f, pl.ds(1, nx), 0, :]
         ypack[1, f] = blk[f, pl.ds(1, nx), ny - 1, :]
     pack_z(4, lambda f, x: blk[f, x + 1], zpack)
-    pl.semaphore_wait(barrier, peers)
-
-    y1 = copies(ypack.at[0], ypack.at[1], yhalo.at[0], yhalo.at[1], 0, send1, recv1, "gy", up_y, down_y)
-    x1 = copies(blk.at[:, 1], blk.at[:, nx], blk.at[:, 0], blk.at[:, nx + 1], 2, send1, recv1, "gx", up_x, down_x)
-    z1 = copies(zpack.at[0], zpack.at[1], zhalo.at[0], zhalo.at[1], 4, send1, recv1, "gz", z_up, z_down)
-    start(z1, None, None)
-    start(y1, not_high_y, not_low_y)
-    start(x1, not_high_x, not_low_x)
-
-    def wall_x(inside, halo_plane, edge_plane):
-        @pl.when(jnp.logical_not(inside))
-        def _():
-            for f in range(3):
-                blk[f, halo_plane] = jnp.zeros((ny, nz), jnp.float32)
-            blk[3, halo_plane] = blk[3, edge_plane]
-
-    wall_x(not_low_x, 0, 1)
-    wall_x(not_high_x, nx + 1, nx)
-
-    def wall_y(inside, side):
-        @pl.when(jnp.logical_not(inside))
-        def _():
-            for f in range(3):
-                yhalo[side, f] = jnp.zeros((nx, nz), jnp.float32)
-            yhalo[side, 3] = ypack[side, 3]
-
-    wall_y(not_low_y, 0)
-    wall_y(not_high_y, 1)
-
     loads[2].wait()
     loads[3].wait()
     loads[4].wait()
@@ -206,11 +177,48 @@
         plane(2 + 2 * i)
         return carry
 
-    lax.fori_loop(0, (nx - 2) // 2, plane_body, 0)
-
     pack_z(1, lambda f, x: void[x], vzpack)
+    early = (nx - 2) // 4
+    lax.fori_loop(0, early, plane_body, 0)
+    pl.semaphore_wait(barrier, peers)
+
+    y1 = copies(ypack.at[0], ypack.at[1], yhalo.at[0], yhalo.at[1], 0, send1, recv1, "gy", up_y, down_y)
+    x1 = copies(blk.at[:, 1], blk.at[:, nx], blk.at[:, 0], blk.at[:, nx + 1], 2, send1, recv1, "gx", up_x, down_x)
+    z1 = copies(zpack.at[0], zpack.at[1], zhalo.at[0], zhalo.at[1], 4, send1, recv1, "gz", z_up, z_down)
+    start(z1, None, None)
+    start(y1, not_high_y, not_low_y)
+    start(x1, not_high_x, not_low_x)
     zv = copies(vzpack.at[0], vzpack.at[1], vzhalo.at[0], vzhalo.at[1], 6, send1, recv1, "gz", z_up, z_down)
     start(zv, None, None)
+
+    spread = len(phases) < len(greet)
+    if spread:
+        for k in range(1, gz):
+            pl.semaphore_signal(
+                entered, inc=1, device_id={"gz": lax.rem(z_at + k, gz)}, device_id_type=MESH)
+
+    def wall_x(inside, halo_plane, edge_plane):
+        @pl.when(jnp.logical_not(inside))
+        def _():
+            for f in range(3):
+                blk[f, halo_plane] = jnp.zeros((ny, nz), jnp.float32)
+            blk[3, halo_plane] = blk[3, edge_plane]
+
+    wall_x(not_low_x, 0, 1)
+    wall_x(not_high_x, nx + 1, nx)
+
+    def wall_y(inside, side):
+        @pl.when(jnp.logical_not(inside))
+        def _():
+            for f in range(3):
+                yhalo[side, f] = jnp.zeros((nx, nz), jnp.float32)
+            yhalo[side, 3] = ypack[side, 3]
+
+    wall_y(not_low_y, 0)
+    wall_y(not_high_y, 1)
+
+    lax.fori_loop(early, (nx - 2) // 2, plane_body, 0)
+
 
     finish(x1, not_high_x, not_low_x)
     plane(0)
@@ -283,6 +291,9 @@
     line = lax.broadcasted_iota(jnp.int32, (1, nz), 1)
     partial = jnp.where(line < nz // 2, fold(flow), fold(void_total))
 
+    if spread:
+        pl.semaphore_wait(entered, gz - 1)
+
     def send_sum(which, value):
         axes = phases[which]
         count = math.prod(lax.axis_size(a) for a in axes)
@@ -333,42 +344,39 @@
         def _():
             fyhalo[side] = jnp.zeros((nx, nz), jnp.float32)
 
+    finish(zv, None, None)
+    vz_joined = join_z(vzhalo)
+
+    def source_plane(x, odd, x_low, x_high):
+        fy, fz, v = flux[1, x], flux[2, x], void[x]
+        y_low = jnp.where(first_row, 0.0, pltpu.roll(fy, 1, 0))
+        y_high = jnp.where(last_row, 0.0, pltpu.roll(fy, ny - 1, 0))
+        v_halo = unpack(vz_joined[odd], x)
+        z_low = jnp.where(first_lane, 0.0, pltpu.roll(fz, 1, 1))
+        z_high = jnp.where(last_lane, 0.0, pltpu.roll(fz, nz - 1, 1))
+        v_low = jnp.where(first_lane, v_halo, pltpu.roll(v, 1, 1))
+        v_high = jnp.where(last_lane, v_halo, pltpu.roll(v, nz - 1, 1))
+        div[x] = 0.5 * ((x_high - x_low) + (y_high - y_low) + (z_high - z_low))
+        slope[x] = (0.5 * time_step) * (v_high - v_low)
+
+    def source_body(i, carry):
+        x = 2 * i + 1
+        source_plane(x, 1, flux[0, x - 1], flux[0, x + 1])
+        source_plane(x + 1, 0, flux[0, x], flux[0, x + 2])
+        return carry
+
+    lax.fori_loop(0, nx // 2 - 1, source_body, 0)
     phase = 0
     while phase < len(phases) - 1:
         total = recv_sum(phase)
         phase += 1
         sent += send_sum(phase, total)
-
     finish(x2, not_high_x, not_low_x)
+    source_plane(0, 0, fxhalo[0], flux[0, 1])
+    source_plane(nx - 1, 1, flux[0, nx - 2], fxhalo[1])
     finish(y2, not_high_y, not_low_y)
     finish(z2, None, None)
-    finish(zv, None, None)
     fz_joined = join_z(fzhalo)
-    vz_joined = join_z(vzhalo)
-
-    def source_plane(x, odd, x_low, x_high):
-        fy, fz, v = flux[1, x], flux[2, x], void[x]
-        y_low = jnp.where(first_row, jnp.broadcast_to(fyhalo[0, pl.ds(x, 1), :], (ny, nz)), pltpu.roll(fy, 1, 0))
-        y_high = jnp.where(last_row, jnp.broadcast_to(fyhalo[1, pl.ds(x, 1), :], (ny, nz)), pltpu.roll(fy, ny - 1, 0))
-        z_halo, v_halo = unpack(fz_joined[odd], x), unpack(vz_joined[odd], x)
-        z_low = jnp.where(first_lane, z_halo, pltpu.roll(fz, 1, 1))
-        z_high = jnp.where(last_lane, z_halo, pltpu.roll(fz, nz - 1, 1))
-        v_low = jnp.where(first_lane, v_halo, pltpu.roll(v, 1, 1))
-        v_high = jnp.where(last_lane, v_halo, pltpu.roll(v, nz - 1, 1))
-        div[x] = 0.5 * ((x_high - x_low) + (y_high - y_low) + (z_high - z_low))
-        slope[x] = (0.5 * time_step) * (v_high - v_low)
-
-    source_plane(0, 0, fxhalo[0], flux[0, 1])
-
-    def source_body(i, carry):
-        x = 2 * i + 1
-        source_plane(x, 1, flux[0, x - 1], flux[0, x + 1])
-        source_plane(x + 1, 0, flux[0, x], flux[0, x + 2])
-        return carry
-
-    lax.fori_loop(0, nx // 2 - 1, source_body, 0)
-    source_plane(nx - 1, 1, flux[0, nx - 2], fxhalo[1])
-
     total = recv_sum(phase)
     half = line < nz // 2
     flow_sum = jnp.sum(jnp.where(half, total, 0.0), axis=1, keepdims=True)
@@ -378,12 +386,22 @@
     step_out[...] = jnp.broadcast_to(step, (1, nz)) + forcing[0]
     step = jnp.broadcast_to(step, (ny, nz))
 
-    def final_body(x, carry):
+    row_half, lane_half = row_sign / time_step, lane_sign / time_step
+
+    def final_plane(x, odd):
         ustar[2, x] = ustar[2, x] + time_step * step
-        div[x] = div[x] + step * slope[x]
+        y_halo = jnp.where(
+            row < ny // 2,
+            jnp.broadcast_to(fyhalo[0, pl.ds(x, 1), :], (ny, nz)),
+            jnp.broadcast_to(fyhalo[1, pl.ds(x, 1), :], (ny, nz)))
+        div[x] = div[x] - row_half * y_halo - lane_half * unpack(fz_joined[odd], x) + step * slope[x]
+
+    def final_body(i, carry):
+        final_plane(2 * i, 0)
+        final_plane(2 * i + 1, 1)
         return carry
 
-    lax.fori_loop(0, nx, final_body, 0, unroll=4)
+    lax.fori_loop(0, nx // 2, final_body, 0, unroll=2)
 
     for copy in sent:
         copy.wait_send()
@@ -395,17 +413,18 @@
 def local(velocity, pressure, voidage, particle_vel, forcing, target_flux):
     nx, ny, nz = voidage.shape
     sizes = tuple(lax.axis_size(a) for a in ("gx", "gy", "gz"))
+    greet = (("gy", "gx"), ("gz",))
     if math.prod(sizes) <= DIRECT_LIMIT:
         phases = (("gz", "gy", "gx"),)
     else:
-        phases = (("gy", "gx"), ("gz",))
+        phases = greet
     slot_count = sum(math.prod(lax.axis_size(a) for a in axes) for axes in phases)
     f32 = jnp.float32
     vmem = pl.BlockSpec(memory_space=pltpu.VMEM)
     hbm = pl.BlockSpec(memory_space=pltpu.HBM)
     dma = pltpu.SemaphoreType.DMA
     vel_new, source, forcing_new = pl.pallas_call(
-        functools.partial(kernel, sizes, phases),
+        functools.partial(kernel, sizes, greet, phases),
         out_shape=(
             pltpu.VMEM((3, nx, ny, nz), f32),
             pltpu.VMEM((nx, ny, nz), f32),
@@ -436,6 +455,7 @@
             pltpu.VMEM((slot_count, 1, nz), f32),
             dma((6,)), dma((8,)), dma((8,)), dma((6,)), dma((6,)),
             dma((slot_count,)), dma((slot_count,)),
+            pltpu.SemaphoreType.REGULAR,
         ],
         compiler_params=pltpu.CompilerParams(collective_id=0, has_side_effects=True),
     )(velocity, pressure, voidage, particle_vel, forcing, target_flux)

time: 24.4 us -> 24 us (0.984)
  Pallas kernels: 19.5 us -> 19.1 us
    pallas_call x1, Pallas kernels: 19.5 us -> 19.1 us  [local(): pl.pallas_call(functools.partial(kernel, sizes, greet, phases), out_shape...]
where the time goes in v3:
time: 24 us; the launch traced here: 23.8 us
  Pallas kernels  19.1 us (80%)
  between operations  3.1 us (13%)
  local copies, waits for them, and re-layouts  1.58 us (7%)
    pallas_call x1, Pallas kernels, local(): pl.pallas_call(functools.partial(kernel, sizes, greet, phases), out_shape...  19.1 us
    unnamed x2, local copies, waits for them, and re-layouts  1.58 us

profile of v3, /device:TPU:0, one launch (start us, length us, event | category | flops | bytes accessed | tf_op | source)
XLA Modules:
  0.0 23.8 jit_solution(272992123712912263)
XLA Ops:
  1.9 19.1 %shard_map.85 = (f32[3,32,16,128]{3,2,1,0:T(8,128)S(1)}, f32[32,16,128]{2,1,0:T(8,128)S(1)}, f32[1,128]{1,0:T(1,128)S(1)}) custom-call(f32[3,32,16,128]{3,2,1,0:T(8,128)} %vel_hbm.1, f32[32,16,128]{2,1,0:T(8,128)} %pres_hbm.1, f32[32,16,128]{2,1,0:T(8,128)} %void_hbm.1, f32[3,32,16,128]{3,2,1,0:T(8,128)} %part_hbm.1, f32[1]{0:T(128)S(6)} %copy.14.forcing_hbm, ...), custom_call_target="tpu_custom_call" | custom-call | tf_op jit(solution)/shard_map/pallas_call | solution.py:426
  21.1 0.9 %copy.12 = f32[3,32,16,128]{3,2,1,0:T(8,128)} copy(f32[3,32,16,128]{3,2,1,0:T(8,128)S(1)} %get-tuple-element.9) | data formatting | bytes 1572864
  21.9 0.7 %copy.13 = f32[32,16,128]{2,1,0:T(8,128)} copy(f32[32,16,128]{2,1,0:T(8,128)S(1)} %get-tuple-element.10) | data formatting | bytes 524288
